TPU v7x, 32 devices: a whole 2x2x4 slice. The times are simulated.
32 devices in a mesh: seq: 8 (over z, y), head: 4 (over x, core).
Axes of the slice: x: 2, y: 2, z: 4, core: 2. Of those that a mesh axis runs over, the one named last changes fastest.
Arguments:
- queries: bfloat16 [1024, 1536], P('seq', 'head'), may hold values from -400 to 400
- latent: bfloat16 [1024, 320], P(('seq', 'head')), may hold values from -6 to 6
- w_kv_up: bfloat16 [256, 2048], P(None, 'head'), may hold values from -0.375 to 0.375
Outputs:
- attended: bfloat16 [1024, 1024], P('seq', 'head')
All inputs are finite; a program needn't handle non-finite values.
Results may differ from a plain program's by a relative error of at most 0.004.
Values may be sent and summed in bfloat16 or wider, within the bound.
A program may use at most 64 MiB of HBM per device.

v0:
```python
import math
import jax
import jax.numpy as jnp
from jax import lax
from jax.sharding import PartitionSpec as P

D_LATENT = 256
ROPE = 64
NOPE = 128
VDIM = 128
MASKED = -1e30


def from_behind(shard, axis, by):
    length = lax.axis_size(axis)
    pairs = [(i, i + by) for i in range(length) if 0 <= i + by < length]
    return lax.ppermute(shard, axis, pairs)


def attend(state, key_block, key_start, setup):
    query_side, query_rope, query_pos, w_kv_up, absorb = setup
    numerator, running_max, totals = state
    local_heads = query_rope.shape[1]
    key_count = key_block.shape[0]
    highest = lax.Precision.HIGHEST
    key_latent = key_block[:, :D_LATENT]
    key_rope = key_block[:, D_LATENT:]
    key_value = jnp.dot(key_latent, w_kv_up, preferred_element_type=jnp.float32)
    key_value = key_value.reshape(key_count, local_heads, NOPE + VDIM)
    scores = jnp.einsum("qhd,khd->hqk", query_side, key_value[:, :, :NOPE], precision=highest)
    scores = scores + jnp.einsum(
        "qhd,kd->hqk", query_rope, key_rope, preferred_element_type=jnp.float32
    )
    scores = scores * (NOPE + ROPE) ** (-0.5)
    key_pos = key_start + lax.iota(jnp.int32, key_count)
    allowed = (key_pos[None, :] <= query_pos[:, None]) & (key_pos[None, :] >= 0)
    scores = jnp.where(allowed[None], scores, MASKED)
    new_max = jnp.maximum(running_max, jnp.max(scores, axis=2))
    factor = jnp.exp(running_max - new_max)
    weights = jnp.where(allowed[None], jnp.exp(scores - new_max[:, :, None]), 0.0)
    totals = totals * factor + jnp.sum(weights, axis=2)
    rounded = weights.astype(jnp.bfloat16)
    update = jnp.einsum(
        "hqk,khd->hqd", rounded.astype(jnp.float32), key_value[:, :, NOPE:], precision=highest
    )
    numerator = numerator * factor[:, :, None] + update
    return (numerator, new_max, totals)


def attend_blocks(state, keys, key_start, setup):
    key_total = keys.shape[0]
    block_rows = key_total if key_total <= 1024 else math.gcd(key_total, 1024)
    block_count = key_total // block_rows

    def one_block(block_index, inner):
        offset = block_index * block_rows
        piece = lax.dynamic_slice_in_dim(keys, offset, block_rows, 0)
        return attend(inner, piece, key_start + offset, setup)

    if block_count == 1:
        return one_block(0, state)
    return lax.fori_loop(0, block_count, one_block, state)


def prepare(query_rows, query_pos, w_kv_up):
    row_count = query_rows.shape[0]
    local_heads = w_kv_up.shape[1] // (NOPE + VDIM)
    query_all = query_rows.reshape(row_count, local_heads, NOPE + ROPE)
    query_side = query_all[:, :, :NOPE].astype(jnp.float32)
    width = VDIM
    setup = (query_side, query_all[:, :, NOPE:], query_pos, w_kv_up, False)
    start_state = (
        jnp.zeros((local_heads, row_count, width), jnp.float32),
        jnp.full((local_heads, row_count), MASKED, jnp.float32),
        jnp.zeros((local_heads, row_count), jnp.float32),
    )
    return (setup, start_state)


def finish(state, w_kv_up):
    numerator, running_max, totals = state
    local_heads = w_kv_up.shape[1] // (NOPE + VDIM)
    row_count = totals.shape[1]
    result = numerator / totals[:, :, None]
    return (
        jnp.transpose(result, (1, 0, 2)).reshape(row_count, local_heads * VDIM).astype(jnp.bfloat16)
    )


def body(queries, latent, w_kv_up):
    group_rows = queries.shape[0]
    seq_groups = lax.axis_size("seq")
    group_index = lax.axis_index("seq")
    query_pos = group_index * group_rows + lax.iota(jnp.int32, group_rows)
    setup, state = prepare(queries, query_pos, w_kv_up)
    gathered = lax.all_gather(latent, "head", axis=0, tiled=True)
    state = attend(state, gathered, group_index * group_rows, setup)
    history = gathered
    span_groups = 1
    while span_groups < seq_groups:
        arrived = from_behind(history, "seq", span_groups)
        state = attend_blocks(
            state, arrived, (group_index - 2 * span_groups + 1) * group_rows, setup
        )
        if 2 * span_groups < seq_groups:
            history = jnp.concatenate([arrived, history], axis=0)
        span_groups = span_groups * 2
    return finish(state, w_kv_up)


def solution(mesh):
    in_specs = (P("seq", "head"), P(("seq", "head"), None), P(None, "head"))
    out_specs = P("seq", "head")
    return jax.shard_map(body, mesh=mesh, in_specs=in_specs, out_specs=out_specs, check_vma=False)
```

profile of v0, /device:TPU:27, one launch (start us, length us, event | category | flops | bytes accessed | tf_op | source)
XLA Modules:
  0.0 42.7 jit_solution(3402798072797051808)
XLA Ops:
  0.0 6.2 %all_gather.3 = bf16[128,320]{1,0:T(8,128)(2,1)S(1)} all-gather(bf16[32,320]{1,0:T(8,128)(2,1)} %param.4), channel_id=1, replica_groups=mesh['seq'=8,'head'=4] {'head'}, dimensions={0}, use_global_device_ids=true | all-gather | bytes 102400 | tf_op jit(solution)/shard_map/all_gather | solution.py:96
  6.3 3.1 %collective-permute-start = (bf16[128,320]{0,1:T(8,128)(2,1)S(1)}, bf16[128,320]{0,1:T(8,128)(2,1)S(1)}, u32[]{:S(2)}, u32[]{:S(2)}) collective-permute-start(bf16[128,320]{0,1:T(8,128)(2,1)S(1)} %copy.39), channel_id=1, source_target_pairs={{0,4},{4,8},{8,12},{12,16},{16,20},{20,24},{24,28},{1,5},{5,9},{9,... | collective-permute-start | bytes 245768 | tf_op jit(solution)/shard_map/ppermute | solution.py:17
  10.4 0.2 compare_and_fusion
  10.7 0.2 fusion.90
  11.1 1.8 %collective-permute-done = bf16[128,320]{0,1:T(8,128)(2,1)S(1)} collective-permute-done((bf16[128,320]{0,1:T(8,128)(2,1)S(1)}, bf16[128,320]{0,1:T(8,128)(2,1)S(1)}, u32[]{:S(2)}, u32[]{:S(2)}) %collective-permute-start) | collective-permute-done | bytes 81952 | tf_op jit(solution)/shard_map/ppermute | solution.py:17
  12.9 1.3 %collective-permute-start.1 = (bf16[256,320]{0,1:T(8,128)(2,1)S(1)}, bf16[256,320]{0,1:T(8,128)(2,1)S(1)}, u32[]{:S(2)}, u32[]{:S(2)}) collective-permute-start(bf16[256,320]{0,1:T(8,128)(2,1)S(1)} %pad_maximum_fusion.1), channel_id=1, source_target_pairs={{0,8},{4,12},{8,16},{12,20},{16,24},{20,28},{1,9},{5,13},{9,17},{1... | collective-permute-start | bytes 491528 | tf_op jit(solution)/shard_map/ppermute | solution.py:17
  14.2 0.2 fusion.51
  14.7 0.2 convolution_bitcast_fusion.7
  14.9 0.2 fusion.89
  15.2 4.4 %collective-permute-done.1 = bf16[256,320]{0,1:T(8,128)(2,1)S(1)} collective-permute-done((bf16[256,320]{0,1:T(8,128)(2,1)S(1)}, bf16[256,320]{0,1:T(8,128)(2,1)S(1)}, u32[]{:S(2)}, u32[]{:S(2)}) %collective-permute-start.1) | collective-permute-done | bytes 163872 | tf_op jit(solution)/shard_map/ppermute | solution.py:17
  19.6 1.3 %collective-permute-start.2 = (bf16[512,320]{0,1:T(8,128)(2,1)S(1)}, bf16[512,320]{0,1:T(8,128)(2,1)S(1)}, u32[]{:S(2)}, u32[]{:S(2)}) collective-permute-start(bf16[512,320]{0,1:T(8,128)(2,1)S(1)} %pad_maximum_fusion), channel_id=1, source_target_pairs={{0,16},{4,20},{8,24},{12,28},{1,17},{5,21},{9,25},{13,29},{2,18},{... | collective-permute-start | bytes 983048 | tf_op jit(solution)/shard_map/ppermute | solution.py:17
  20.9 0.2 fusion.36
  21.2 0.3 reshape.300
  21.7 0.2 convolution_bitcast_fusion.2
  21.9 0.2 fusion.88
  22.2 16.7 %collective-permute-done.2 = bf16[512,320]{0,1:T(8,128)(2,1)S(1)} collective-permute-done((bf16[512,320]{0,1:T(8,128)(2,1)S(1)}, bf16[512,320]{0,1:T(8,128)(2,1)S(1)}, u32[]{:S(2)}, u32[]{:S(2)}) %collective-permute-start.2) | collective-permute-done | bytes 327712 | tf_op jit(solution)/shard_map/ppermute | solution.py:17
  38.9 0.3 fusion.26
  39.3 0.6 %convolution_bitcast_fusion.1 = f32[2,128,512]{1,2,0:T(8,128)S(1)} fusion(f32[512,2,256]{0,2,1:T(8,128)S(1)} %bitcast.164, bf16[128,2,192]{0,2,1:T(8,128)(2,1)S(1)} %bitcast.162), kind=kOutput, calls=%fused_computation.2 | convolution fusion | flops 201326592 | bytes 1114112 | tf_op jit(solution)/shard_map/qhd,khd->hqk/dot_general | solution.py:30
  39.9 0.3 fusion.87
  40.5 0.3 fusion.15
  40.8 0.3 fusion.16
  41.1 0.4 %fusion.9 = f32[128,2,128]{0,2,1:T(8,128)S(1)} fusion(f32[128,2,128]{0,2,1:T(8,128)S(1)} %fusion.16, f32[256,2,128]{2,1,0:T(2,128)S(1)} %get-tuple-element.11, f32[2,128,256]{1,2,0:T(8,128)S(1)} %get-tuple-element.25, f32[2,128]{1,0:T(2,128)S(1)} %get-tuple-element.9, pred[128,256]{0,1:T(8,128)(4,1)S(1)} %compare_and_fusion.1, ...), kind=kOutput, calls=%fused_computation.15 | convolution fusion | flops 100925440 | bytes 821248 | tf_op jit(solution)/shard_map/hqk,khd->hqd/dot_general | solution.py:43
  41.5 0.4 %fusion.20 = bf16[128,2,128]{0,2,1:T(8,128)(2,1)S(1)} fusion(f32[128,2,128]{0,2,1:T(8,128)S(1)} %fusion.9, f32[512,2,256]{0,2,1:T(8,128)S(1)} %bitcast.165, f32[2,128,512]{1,2,0:T(8,128)S(1)} %get-tuple-element.23, f32[2,128]{1,0:T(2,128)S(1)} %get-tuple-element.8, pred[128,512]{0,1:T(8,128)(4,1)S(1)} %compare_and_fusion, f32[128,2]{0,1:T(2,128)S(1)} %get-tuple-element.5), kind=kOutput, calls=%fused_computation.32 | convolution fusion | flops 201818112 | bytes 1312768 | tf_op jit(solution)/shard_map/hqk,khd->hqd/dot_general | solution.py:43
  42.0 0.7 %copy.53 = bf16[128,256]{1,0:T(8,128)(2,1)} copy(bf16[128,256]{0,1:T(8,128)(2,1)S(1)} %bitcast.166) | data formatting | bytes 131072 | tf_op jit(solution)/shard_map/convert_element_type | solution.py:86
  (30 shorter events, 2.0 us)
Async XLA Ops:
  0.0 9.9 %copy-start = (bf16[256,512]{1,0:T(8,128)(2,1)S(1)}, bf16[256,512]{1,0:T(8,128)(2,1)}, u32[]{:S(2)}) copy-start(bf16[256,512]{1,0:T(8,128)(2,1)} %param.5) | copy-start | bytes 786436
  6.2 3.4 %copy-start.1 = (bf16[128,384]{1,0:T(8,128)(2,1)S(1)}, bf16[128,384]{1,0:T(8,128)(2,1)}, u32[]{:S(2)}) copy-start(bf16[128,384]{1,0:T(8,128)(2,1)} %param.3) | copy-start | bytes 294916
  6.3 6.6 %collective-permute-start = (bf16[128,320]{0,1:T(8,128)(2,1)S(1)}, bf16[128,320]{0,1:T(8,128)(2,1)S(1)}, u32[]{:S(2)}, u32[]{:S(2)}) collective-permute-start(bf16[128,320]{0,1:T(8,128)(2,1)S(1)} %copy.39), channel_id=1, source_target_pairs={{0,4},{4,8},{8,12},{12,16},{16,20},{20,24},{24,28},{1,5},{5,9},{9,... | collective-permute-start | bytes 245768 | tf_op jit(solution)/shard_map/ppermute | solution.py:17
  12.9 6.6 %collective-permute-start.1 = (bf16[256,320]{0,1:T(8,128)(2,1)S(1)}, bf16[256,320]{0,1:T(8,128)(2,1)S(1)}, u32[]{:S(2)}, u32[]{:S(2)}) collective-permute-start(bf16[256,320]{0,1:T(8,128)(2,1)S(1)} %pad_maximum_fusion.1), channel_id=1, source_target_pairs={{0,8},{4,12},{8,16},{12,20},{16,24},{20,28},{1,9},{5,13},{9,17},{1... | collective-permute-start | bytes 491528 | tf_op jit(solution)/shard_map/ppermute | solution.py:17
  19.6 19.3 %collective-permute-start.2 = (bf16[512,320]{0,1:T(8,128)(2,1)S(1)}, bf16[512,320]{0,1:T(8,128)(2,1)S(1)}, u32[]{:S(2)}, u32[]{:S(2)}) collective-permute-start(bf16[512,320]{0,1:T(8,128)(2,1)S(1)} %pad_maximum_fusion), channel_id=1, source_target_pairs={{0,16},{4,20},{8,24},{12,28},{1,17},{5,21},{9,25},{13,29},{2,18},{... | collective-permute-start | bytes 983048 | tf_op jit(solution)/shard_map/ppermute | solution.py:17
where the time goes:
time: 42.9 us; the launch traced here: 42.7 us
  waiting for transfers between devices  23 us (54%)
  blocking collectives  6.16 us (14%)
  starting transfers between devices  5.73 us (13%)
  matrix products  4.62 us (11%)
  local copies, waits for them, and re-layouts  2.04 us (5%)
  other arithmetic  0.87 us (2%)
    ppermute x3, waiting for transfers between devices, from_behind(): return lax.ppermute(shard, axis, pairs)  23 us
    all_gather x1, blocking collectives, body(): gathered = lax.all_gather(latent, 'head', axis=0, tiled=True)  6.16 us
    ppermute x3, starting transfers between devices, from_behind(): return lax.ppermute(shard, axis, pairs)  5.73 us
    dot_general x4, matrix products, attend(): jnp.einsum('hqk,khd->hqd', rounded.astype(jnp.float32), key_value[:, :, N...  1.46 us
    dot_general x4, matrix products, attend(): jnp.einsum('qhd,khd->hqk', query_side, key_value[:, :, :NOPE], precision=...  1.25 us
    dot_general x4, matrix products, attend(): key_value = jnp.dot(key_latent, w_kv_up, preferred_element_type=jnp.float32)  0.97 us
    dot_general x4, matrix products, attend(): jnp.einsum('qhd,kd->hqk', query_rope, key_rope, preferred_element_type=jn...  0.94 us
  transfers between devices with their start and end apart: 3, of which 3 were waited for; matrix products, arithmetic and copies ran while one was open for 9% of the time, Pallas kernels for 0%

commit v1 on v0

--- a/solution.py
+++ b/solution.py
@@ -93,7 +93,12 @@
     group_index = lax.axis_index("seq")
     query_pos = group_index * group_rows + lax.iota(jnp.int32, group_rows)
     setup, state = prepare(queries, query_pos, w_kv_up)
-    gathered = lax.all_gather(latent, "head", axis=0, tiled=True)
+    ring = [latent]
+    for hop in range(3):
+        ring.append(lax.ppermute(ring[-1], "head", [(dev, (dev + 1) % 4) for dev in range(4)]))
+    gathered = jnp.roll(
+        jnp.concatenate(ring[::-1], axis=0), (lax.axis_index("head") + 1) * ring[0].shape[0], axis=0
+    )
     state = attend(state, gathered, group_index * group_rows, setup)
     history = gathered
     span_groups = 1

time: 42.9 us -> 47.6 us (1.11)
  the two profiles are of different devices: /device:TPU:27 before, /device:TPU:24 now
where the time goes in v1:
time: 47.6 us; the launch traced here: 47.4 us
  waiting for transfers between devices  32.2 us (68%)
  starting transfers between devices  6.07 us (13%)
  matrix products  4.81 us (10%)
  local copies, waits for them, and re-layouts  3.17 us (7%)
  other arithmetic  0.88 us (2%)
    ppermute x3, waiting for transfers between devices, from_behind(): return lax.ppermute(shard, axis, pairs)  21.4 us
    ppermute x3, waiting for transfers between devices, body(): lax.ppermute(ring[-1], 'head', [(dev, (dev + 1) % 4) for dev in range(4)])  10.8 us
    ppermute x3, starting transfers between devices, from_behind(): return lax.ppermute(shard, axis, pairs)  6.01 us
    dot_general x4, matrix products, attend(): jnp.einsum('hqk,khd->hqd', rounded.astype(jnp.float32), key_value[:, :, N...  1.46 us
    dot_general x4, matrix products, attend(): jnp.einsum('qhd,khd->hqk', query_side, key_value[:, :, :NOPE], precision=...  1.23 us
    dot_general x4, matrix products, attend(): key_value = jnp.dot(key_latent, w_kv_up, preferred_element_type=jnp.float32)  1.07 us
    dot_general x4, matrix products, attend(): jnp.einsum('qhd,kd->hqk', query_rope, key_rope, preferred_element_type=jn...  1.04 us
    unnamed x6, local copies, waits for them, and re-layouts  1.03 us
  transfers between devices with their start and end apart: 6, of which 6 were waited for; matrix products, arithmetic and copies ran while one was open for 8% of the time, Pallas kernels for 0%

profile of v1, /device:TPU:24, one launch (start us, length us, event | category | flops | bytes accessed | tf_op | source)
XLA Modules:
  0.0 47.4 jit_solution(10608796393248915365)
XLA Ops:
  0.0 0.9 %copy.23 = bf16[32,320]{0,1:T(8,128)(2,1)S(1)} copy(bf16[32,320]{1,0:T(8,128)(2,1)} %param.4) | data formatting | bytes 40960 | tf_op args[1]
  1.4 3.4 %collective-permute-done = bf16[32,320]{0,1:T(8,128)(2,1)S(1)} collective-permute-done((bf16[32,320]{0,1:T(8,128)(2,1)S(1)}, bf16[32,320]{0,1:T(8,128)(2,1)S(1)}, u32[]{:S(2)}, u32[]{:S(2)}) %collective-permute-start) | collective-permute-done | bytes 20512 | tf_op jit(solution)/shard_map/ppermute | solution.py:98
  4.8 3.9 %collective-permute-done.1 = bf16[32,320]{0,1:T(8,128)(2,1)S(1)} collective-permute-done((bf16[32,320]{0,1:T(8,128)(2,1)S(1)}, bf16[32,320]{0,1:T(8,128)(2,1)S(1)}, u32[]{:S(2)}, u32[]{:S(2)}) %collective-permute-start.1) | collective-permute-done | bytes 20512 | tf_op jit(solution)/shard_map/ppermute | solution.py:98
  9.0 3.6 %collective-permute-done.2 = bf16[32,320]{0,1:T(8,128)(2,1)S(1)} collective-permute-done((bf16[32,320]{0,1:T(8,128)(2,1)S(1)}, bf16[32,320]{0,1:T(8,128)(2,1)S(1)}, u32[]{:S(2)}, u32[]{:S(2)}) %collective-permute-start.2) | collective-permute-done | bytes 20512 | tf_op jit(solution)/shard_map/ppermute | solution.py:98
  12.6 0.2 concatenate.13
  12.9 3.4 %collective-permute-start.3 = (bf16[128,320]{0,1:T(8,128)(2,1)S(1)}, bf16[128,320]{0,1:T(8,128)(2,1)S(1)}, u32[]{:S(2)}, u32[]{:S(2)}) collective-permute-start(bf16[128,320]{0,1:T(8,128)(2,1)S(1)} %constant_dynamic-slice_fusion), channel_id=1, source_target_pairs={{0,4},{4,8},{8,12},{12,16},{16,20},{20,24},{24,28},{1,5},{5,9},{9,... | collective-permute-start | bytes 245768 | tf_op jit(solution)/shard_map/ppermute | solution.py:17
  16.4 0.3 fusion.53
  17.1 0.3 fusion.91
  17.4 2.7 %collective-permute-done.3 = bf16[128,320]{0,1:T(8,128)(2,1)S(1)} collective-permute-done((bf16[128,320]{0,1:T(8,128)(2,1)S(1)}, bf16[128,320]{0,1:T(8,128)(2,1)S(1)}, u32[]{:S(2)}, u32[]{:S(2)}) %collective-permute-start.3) | collective-permute-done | bytes 81952 | tf_op jit(solution)/shard_map/ppermute | solution.py:17
  20.2 1.3 %collective-permute-start.4 = (bf16[256,320]{0,1:T(8,128)(2,1)S(1)}, bf16[256,320]{0,1:T(8,128)(2,1)S(1)}, u32[]{:S(2)}, u32[]{:S(2)}) collective-permute-start(bf16[256,320]{0,1:T(8,128)(2,1)S(1)} %pad_maximum_fusion.1), channel_id=1, source_target_pairs={{0,8},{4,12},{8,16},{12,20},{16,24},{20,28},{1,9},{5,13},{9,17},{1... | collective-permute-start | bytes 491528 | tf_op jit(solution)/shard_map/ppermute | solution.py:17
  22.4 5.0 %collective-permute-done.4 = bf16[256,320]{0,1:T(8,128)(2,1)S(1)} collective-permute-done((bf16[256,320]{0,1:T(8,128)(2,1)S(1)}, bf16[256,320]{0,1:T(8,128)(2,1)S(1)}, u32[]{:S(2)}, u32[]{:S(2)}) %collective-permute-start.4) | collective-permute-done | bytes 163872 | tf_op jit(solution)/shard_map/ppermute | solution.py:17
  27.4 1.3 %collective-permute-start.5 = (bf16[512,320]{0,1:T(8,128)(2,1)S(1)}, bf16[512,320]{0,1:T(8,128)(2,1)S(1)}, u32[]{:S(2)}, u32[]{:S(2)}) collective-permute-start(bf16[512,320]{0,1:T(8,128)(2,1)S(1)} %pad_maximum_fusion), channel_id=1, source_target_pairs={{0,16},{4,20},{8,24},{12,28},{1,17},{5,21},{9,25},{13,29},{2,18},{... | collective-permute-start | bytes 983048 | tf_op jit(solution)/shard_map/ppermute | solution.py:17
  29.0 0.3 reshape.300
  29.5 0.2 convolution_bitcast_fusion.2
  29.8 0.2 fusion.89
  30.0 13.7 %collective-permute-done.5 = bf16[512,320]{0,1:T(8,128)(2,1)S(1)} collective-permute-done((bf16[512,320]{0,1:T(8,128)(2,1)S(1)}, bf16[512,320]{0,1:T(8,128)(2,1)S(1)}, u32[]{:S(2)}, u32[]{:S(2)}) %collective-permute-start.5) | collective-permute-done | bytes 327712 | tf_op jit(solution)/shard_map/ppermute | solution.py:17
  43.7 0.3 fusion.26
  44.0 0.6 %convolution_bitcast_fusion.1 = f32[2,128,512]{1,2,0:T(8,128)S(1)} fusion(f32[512,2,256]{0,2,1:T(8,128)S(1)} %bitcast.166, bf16[128,2,192]{0,2,1:T(8,128)(2,1)S(1)} %bitcast.164), kind=kOutput, calls=%fused_computation.2 | convolution fusion | flops 201326592 | bytes 1114112 | tf_op jit(solution)/shard_map/qhd,khd->hqk/dot_general | solution.py:30
  44.6 0.3 fusion.88
  45.2 0.3 fusion.12
  45.5 0.3 fusion.13
  45.8 0.4 fusion.9
  46.3 0.4 fusion.20
  46.7 0.7 %copy.39 = bf16[128,256]{1,0:T(8,128)(2,1)} copy(bf16[128,256]{0,1:T(8,128)(2,1)S(1)} %bitcast.168) | data formatting | bytes 131072 | tf_op jit(solution)/shard_map/convert_element_type | solution.py:86
  (37 shorter events, 2.9 us)
Async XLA Ops:
  0.0 16.4 %copy-start = (bf16[256,512]{1,0:T(8,128)(2,1)S(1)}, bf16[256,512]{1,0:T(8,128)(2,1)}, u32[]{:S(2)}) copy-start(bf16[256,512]{1,0:T(8,128)(2,1)} %param.5) | copy-start | bytes 786436
  0.9 3.9 %collective-permute-start = (bf16[32,320]{0,1:T(8,128)(2,1)S(1)}, bf16[32,320]{0,1:T(8,128)(2,1)S(1)}, u32[]{:S(2)}, u32[]{:S(2)}) collective-permute-start(bf16[32,320]{0,1:T(8,128)(2,1)S(1)} %copy.23), channel_id=1, source_target_pairs={{0,1},{1,2},{2,3},{3,0},{4,5},{5,6},{6,7},{7,4},{8,9},{9,10},{10,1... | collective-permute-start | bytes 61448 | tf_op jit(solution)/shard_map/ppermute | solution.py:98
  1.0 7.8 %copy-start.1 = (bf16[128,384]{1,0:T(8,128)(2,1)S(1)}, bf16[128,384]{1,0:T(8,128)(2,1)}, u32[]{:S(2)}) copy-start(bf16[128,384]{1,0:T(8,128)(2,1)} %param.3) | copy-start | bytes 294916
  4.8 3.9 %collective-permute-start.1 = (bf16[32,320]{0,1:T(8,128)(2,1)S(1)}, bf16[32,320]{0,1:T(8,128)(2,1)S(1)}, u32[]{:S(2)}, u32[]{:S(2)}) collective-permute-start(bf16[32,320]{0,1:T(8,128)(2,1)S(1)} %collective-permute-done), channel_id=1, source_target_pairs={{0,1},{1,2},{2,3},{3,0},{4,5},{5,6},{6,7},{7,4},{8,9},{9,10},{10,1... | collective-permute-start | bytes 61448 | tf_op jit(solution)/shard_map/ppermute | solution.py:98
  8.7 3.9 %collective-permute-start.2 = (bf16[32,320]{0,1:T(8,128)(2,1)S(1)}, bf16[32,320]{0,1:T(8,128)(2,1)S(1)}, u32[]{:S(2)}, u32[]{:S(2)}) collective-permute-start(bf16[32,320]{0,1:T(8,128)(2,1)S(1)} %collective-permute-done.1), channel_id=1, source_target_pairs={{0,1},{1,2},{2,3},{3,0},{4,5},{5,6},{6,7},{7,4},{8,9},{9,10},{10,1... | collective-permute-start | bytes 61448 | tf_op jit(solution)/shard_map/ppermute | solution.py:98
  12.9 7.2 %collective-permute-start.3 = (bf16[128,320]{0,1:T(8,128)(2,1)S(1)}, bf16[128,320]{0,1:T(8,128)(2,1)S(1)}, u32[]{:S(2)}, u32[]{:S(2)}) collective-permute-start(bf16[128,320]{0,1:T(8,128)(2,1)S(1)} %constant_dynamic-slice_fusion), channel_id=1, source_target_pairs={{0,4},{4,8},{8,12},{12,16},{16,20},{20,24},{24,28},{1,5},{5,9},{9,... | collective-permute-start | bytes 245768 | tf_op jit(solution)/shard_map/ppermute | solution.py:17
  20.2 7.2 %collective-permute-start.4 = (bf16[256,320]{0,1:T(8,128)(2,1)S(1)}, bf16[256,320]{0,1:T(8,128)(2,1)S(1)}, u32[]{:S(2)}, u32[]{:S(2)}) collective-permute-start(bf16[256,320]{0,1:T(8,128)(2,1)S(1)} %pad_maximum_fusion.1), channel_id=1, source_target_pairs={{0,8},{4,12},{8,16},{12,20},{16,24},{20,28},{1,9},{5,13},{9,17},{1... | collective-permute-start | bytes 491528 | tf_op jit(solution)/shard_map/ppermute | solution.py:17
  27.4 16.2 %collective-permute-start.5 = (bf16[512,320]{0,1:T(8,128)(2,1)S(1)}, bf16[512,320]{0,1:T(8,128)(2,1)S(1)}, u32[]{:S(2)}, u32[]{:S(2)}) collective-permute-start(bf16[512,320]{0,1:T(8,128)(2,1)S(1)} %pad_maximum_fusion), channel_id=1, source_target_pairs={{0,16},{4,20},{8,24},{12,28},{1,17},{5,21},{9,25},{13,29},{2,18},{... | collective-permute-start | bytes 983048 | tf_op jit(solution)/shard_map/ppermute | solution.py:17
